TPU v7x, 32 devices: a whole 2x2x4 slice. The times are simulated.
32 devices in a mesh: grp: 16 (over z, y, core), tp: 2 (over x).
Axes of the slice: x: 2, y: 2, z: 4, core: 2. Of those that a mesh axis runs over, the one named last changes fastest.
Arguments:
- tokens: bfloat16 [1024, 6144], P('grp', 'tp'), may hold values from -6 to 6
- norm_gain: float32 [6144], replicated, may hold values from 0.25 to 1.75
- router_weight: bfloat16 [6144, 8], replicated, may hold values from -0.078125 to 0.078125
- expert_ids: int32 [1024, 2], P('grp'), may hold values from 0 to 7, all different within a row; in each aligned block of 64 rows (0 to 63, 64 to 127, ...) at most 18 rows name the same one
- gate_proj: bfloat16 [6144, 65536], P(None, ('grp', 'tp')), may hold values from -0.078125 to 0.078125
- up_proj: bfloat16 [6144, 65536], P(None, ('grp', 'tp')), may hold values from -0.078125 to 0.078125
- down_proj: bfloat16 [65536, 6144], P(('grp', 'tp')), may hold values from -0.125 to 0.125
Outputs:
- mixed: bfloat16 [1024, 6144], P('grp', 'tp')
Inputs may be any that keep to these rules, and one draw needn't show every extreme that they name: `expert_ids`: each row names two different experts; within the rows of one group (aligned blocks of 64 rows) no expert is named more than 18 times, and in some group one expert is named exactly 18 times.
All inputs are finite; a program needn't handle non-finite values.
Results may differ from a plain program's by a relative error of at most 0.017.
Values may be sent and summed in bfloat16 or wider, within the bound.
A program may use at most 128 MiB of HBM per device.

v0:
```python
from functools import partial

import jax
import jax.numpy as jnp
from jax import lax
from jax.sharding import PartitionSpec as P

CAP = 18


epsilon = 1e-05


def expert_rows(gate_proj, up_proj, down_proj, gather_first, received):
    source_groups, slot_count, feature_width = received.shape
    row_block = received.reshape(source_groups * slot_count, feature_width)
    gate_act = jnp.dot(row_block, gate_proj, preferred_element_type=jnp.float32)
    up_act = jnp.dot(row_block, up_proj, preferred_element_type=jnp.float32)
    hidden = (jax.nn.silu(gate_act) * up_act).astype(jnp.bfloat16)
    partial_out = jnp.dot(hidden, down_proj, preferred_element_type=jnp.float32).astype(
        jnp.bfloat16
    )
    partial_out = partial_out.reshape(source_groups, slot_count, feature_width)
    own_share = (
        lax.psum_scatter(partial_out, "tp", scatter_dimension=2, tiled=True)
        .astype(jnp.float32)
        .astype(jnp.bfloat16)
    )
    return lax.all_to_all(own_share, "grp", split_axis=0, concat_axis=0, tiled=True)


def per_device(tokens, norm_gain, router_weight, expert_ids, gate_proj, up_proj, down_proj):
    tok_rows, local_width = tokens.shape
    experts = router_weight.shape[1]
    groups = lax.axis_size("grp")
    owners = groups // experts
    capacity = CAP
    whole_rows = lax.all_gather(tokens, "tp", axis=1, tiled=True).astype(jnp.float32)
    mean_square = jnp.mean(whole_rows * whole_rows, axis=-1, keepdims=True)
    normed = (whole_rows * lax.rsqrt(mean_square + epsilon) * norm_gain).astype(jnp.bfloat16)
    logits = jnp.dot(normed, router_weight, preferred_element_type=jnp.float32)
    expert_iota = jnp.arange(experts, dtype=jnp.int32)[None, :]
    chosen_first = (expert_ids[:, 0:1] == expert_iota).astype(jnp.int32)
    chosen_second = (expert_ids[:, 1:2] == expert_iota).astype(jnp.int32)
    first_logit = jnp.sum(logits * chosen_first.astype(jnp.float32), axis=-1)
    second = jnp.sum(logits * chosen_second.astype(jnp.float32), axis=-1)
    gate_first = 1.0 / (1.0 + jnp.exp(second - first_logit))
    gate_second = 1.0 / (1.0 + jnp.exp(first_logit - second))
    gate_table = gate_first[:, None] * chosen_first.astype(jnp.float32) + gate_second[
        :, None
    ] * chosen_second.astype(jnp.float32)
    routed = chosen_first + chosen_second
    slot_index = jnp.cumsum(routed, axis=0) - 1
    slot_iota = jnp.arange(capacity, dtype=jnp.int32)
    slot_picks = (slot_index.T[:, None, :] == slot_iota[None, :, None]) & (
        routed.T[:, None, :] == 1
    )
    selector = slot_picks.astype(jnp.bfloat16)
    per_expert = jnp.einsum(
        "ect,td->ecd", selector, normed, preferred_element_type=jnp.float32
    ).astype(jnp.bfloat16)
    outgoing = jnp.repeat(per_expert, owners, axis=0)
    worker = partial(expert_rows, gate_proj, up_proj, down_proj, False)
    returned = worker(lax.all_to_all(outgoing, "grp", split_axis=0, concat_axis=0, tiled=True))
    summed = (
        returned.astype(jnp.float32).reshape(experts, owners, capacity, local_width).sum(axis=1)
    )
    combine = slot_picks.astype(jnp.float32) * gate_table.T[:, None, :]
    mixed = jnp.einsum("ect,ecd->td", combine, summed, precision=lax.Precision.HIGHEST)
    return mixed.astype(jnp.bfloat16)


def solution(mesh):
    in_specs = (
        P("grp", "tp"),
        P(),
        P(),
        P("grp", None),
        P(None, ("grp", "tp")),
        P(None, ("grp", "tp")),
        P(("grp", "tp"), None),
    )
    out_specs = P("grp", "tp")
    return jax.shard_map(
        per_device, mesh=mesh, in_specs=in_specs, out_specs=out_specs, check_vma=False
    )
```

profile of v0, /device:TPU:13, one launch (start us, length us, event | category | flops | bytes accessed | tf_op | source)
XLA Modules:
  0.0 308.8 jit_solution(13119897074421814599)
XLA Ops:
  6.5 0.0 copy-start
  6.5 0.0 reduce-scatter.2.cloned.1.call-start
  6.5 0.8 slice_bitcast_fusion.1
  7.3 0.1 copy.10
  7.4 0.1 reduce_window_sum.11
  7.5 0.1 copy.11
  7.6 10.9 %all_gather.3 = bf16[64,6144]{1,0:T(8,128)(2,1)S(1)} all-gather(bf16[64,3072]{1,0:T(8,128)(2,1)} %param.7), channel_id=1, replica_groups=mesh['grp'=16,'tp'=2] {'tp'}, dimensions={1}, use_global_device_ids=true | all-gather | bytes 1179648 | tf_op jit(solution)/shard_map/all_gather | solution.py:38
  18.4 0.3 fusion.7
  18.7 1.6 convolution_convert_fusion.1
  20.3 0.6 broadcast_in_dim.2
  20.9 110.7 %all_to_all.10 = bf16[16,18,6144]{2,1,0:T(8,128)(2,1)} all-to-all(bf16[16,18,6144]{2,1,0:T(8,128)(2,1)S(1)} %bitcast.24), channel_id=1, replica_groups=mesh['grp'=16,'tp'=2] {'grp'}, dimensions={0} | all-to-all | bytes 7077888 | tf_op jit(solution)/shard_map/all_to_all | solution.py:64
  131.6 5.1 %reshape.148 = bf16[288,6144]{1,0:T(8,128)(2,1)} reshape(bf16[16,18,6144]{2,1,0:T(8,128)(2,1)} %all_to_all.10) | data formatting | bytes 7077888 | tf_op jit(solution)/shard_map/reshape | solution.py:16
  136.7 13.2 %fusion.35 = f32[288,2048]{1,0:T(8,128)S(1)} fusion(bf16[288,6144]{1,0:T(8,128)(2,1)} %reshape.148, bf16[6144,2048]{1,0:T(8,128)(2,1)} %param.11), kind=kOutput, calls=%fused_computation.55 | convolution fusion | flops 7247757312 | bytes 31064064 | tf_op jit(solution)/shard_map/dot_general | solution.py:17
  150.0 24.5 %convolution_convert_fusion = bf16[288,6144]{1,0:T(8,128)(2,1)} fusion(bf16[2048,6144]{1,0:T(8,128)(2,1)} %param.13, bf16[288,6144]{1,0:T(8,128)(2,1)} %reshape.148, bf16[6144,2048]{1,0:T(8,128)(2,1)} %param.12, f32[288,2048]{1,0:T(8,128)S(1)} %fusion.35), kind=kOutput, calls=%fused_computation | convolution fusion | flops 14500823040 | bytes 59768832 | tf_op jit(solution)/shard_map/dot_general | solution.py:20
  174.5 5.1 %reshape.149 = bf16[16,18,6144]{2,1,0:T(8,128)(2,1)} reshape(bf16[288,6144]{1,0:T(8,128)(2,1)} %convolution_convert_fusion) | data formatting | bytes 7077888 | tf_op jit(solution)/shard_map/reshape | solution.py:23
  179.6 0.0 reduce-scatter.2.cloned.1.call-update
  179.6 0.0 copy-start.1
  179.7 59.9 %reduce-scatter.2.cloned.1.call-done = bf16[16,18,3072]{2,1,0:T(8,128)(2,1)} async-done(((bf16[16,18,6144]{2,1,0:T(8,128)(2,1)}), bf16[16,18,3072]{2,1,0:T(8,128)(2,1)}) %reduce-scatter.2.cloned.1.call-update) | async-done | bytes 1769488 | tf_op jit(solution)/shard_map/reduce_scatter | solution.py:25
  239.6 6.5 %all-to-all-start.1 = ((bf16[16,18,3072]{2,1,0:T(8,128)(2,1)}), bf16[16,18,3072]{2,1,0:T(8,128)(2,1)S(1)}, u32[]{:S(2)}, u32[]{:S(2)}) async-start(bf16[16,18,3072]{2,1,0:T(8,128)(2,1)} %reduce-scatter.2.cloned.1.call-done), calls=%async_computation.2 | async-start | bytes 4718592 | tf_op jit(solution)/shard_map/all_to_all | solution.py:29
  246.1 0.0 copy-done
  246.1 0.0 copy-done.1
  246.1 0.4 fusion.28
  246.5 52.6 %all-to-all-done.1 = bf16[16,18,3072]{2,1,0:T(8,128)(2,1)S(1)} async-done(((bf16[16,18,3072]{2,1,0:T(8,128)(2,1)}), bf16[16,18,3072]{2,1,0:T(8,128)(2,1)S(1)}, u32[]{:S(2)}, u32[]{:S(2)}) %all-to-all-start.1) | async-done | bytes 1769504 | tf_op jit(solution)/shard_map/all_to_all | solution.py:29
  299.1 0.5 convert_reduce_fusion
  299.6 2.4 fusion
  (6 shorter events, 0.1 us)
Async XLA Ops:
  6.5 239.6 %copy-start = (bf16[6144,8]{0,1:T(8,128)(2,1)S(1)}, bf16[6144,8]{0,1:T(8,128)(2,1)}, u32[]{:S(2)}) copy-start(bf16[6144,8]{0,1:T(8,128)(2,1)} %param.9) | copy-start | bytes 294916
  6.5 233.0 %reduce-scatter.2.cloned.1.call-start = ((), (), s32[]{:S(2)}) async-start(), calls=%async_computation.3 | async-start | bytes 7077888 | tf_op jit(solution)/shard_map/reduce_scatter | solution.py:25
  179.6 66.5 %copy-start.1 = (f32[6144]{0:T(1024)S(1)}, f32[6144]{0:T(1024)}, u32[]{:S(2)}) copy-start(f32[6144]{0:T(1024)} %param.8) | copy-start | bytes 73732
  239.6 59.5 %all-to-all-start.1 = ((bf16[16,18,3072]{2,1,0:T(8,128)(2,1)}), bf16[16,18,3072]{2,1,0:T(8,128)(2,1)S(1)}, u32[]{:S(2)}, u32[]{:S(2)}) async-start(bf16[16,18,3072]{2,1,0:T(8,128)(2,1)} %reduce-scatter.2.cloned.1.call-done), calls=%async_computation.2 | async-start | bytes 4718592 | tf_op jit(solution)/shard_map/all_to_all | solution.py:29
Sparse Core Ops, SparseCore 0:
  179.8 59.7 reduce-scatter.1
where the time goes:
time: 309 us
  blocking collectives  122 us (39%)
  waiting for transfers between devices  113 us (37%)
  matrix products  42.1 us (14%)
  between operations  13.5 us (4%)
  local copies, waits for them, and re-layouts  11.7 us (4%)
  starting transfers between devices  6.51 us (2%)
    all_to_all x1, blocking collectives, per_device(): lax.all_to_all(outgoing, 'grp', split_axis=0, concat_axis=0, tiled=True)  111 us
    reduce_scatter x1, waiting for transfers between devices, expert_rows(): lax.psum_scatter(partial_out, 'tp', scatter_dimension=2, tiled=True)  59.9 us
    all_to_all x1, waiting for transfers between devices, expert_rows(): lax.all_to_all(own_share, 'grp', split_axis=0, concat_axis=0, tiled=True)  52.6 us
    dot_general x1, matrix products, expert_rows(): jnp.dot(hidden, down_proj, preferred_element_type=jnp.float32)  24.5 us
    dot_general x1, matrix products, expert_rows(): gate_act = jnp.dot(row_block, gate_proj, preferred_element_type=jnp.float32)  13.2 us
    all_gather x1, blocking collectives, per_device(): lax.all_gather(tokens, 'tp', axis=1, tiled=True).astype(jnp.float32)  10.9 us
    all_to_all x1, starting transfers between devices, expert_rows(): lax.all_to_all(own_share, 'grp', split_axis=0, concat_axis=0, tiled=True)  6.51 us
  transfers between devices with their start and end apart: 2, of which 2 were waited for; matrix products, arithmetic and copies ran while one was open for 0% of the time, Pallas kernels for 0%

commit v1 on v0

v1 whole, which is shorter than its diff:
```python
from functools import partial

import jax
import jax.numpy as jnp
from jax import lax
from jax.experimental import pallas as pl
from jax.experimental.pallas import tpu as pltpu
from jax.sharding import PartitionSpec as P

CAP = 18
MESH = pl.DeviceIdType.MESH


epsilon = 1e-05


def place(experts, owners, pieces):
    g, p = lax.axis_index("grp"), lax.axis_index("tp")
    return g, p, g // owners, lax.rem(g, owners)


def greet(experts, owners, pieces):
    g, p, c, k = place(experts, owners, pieces)
    barrier = pltpu.get_barrier_semaphore()
    peers = [(lax.rem(c + j, experts) * owners + k, p) for j in range(1, experts)]
    peers += [(c * owners + lax.rem(k + d, owners), p) for d in range(1, owners)]
    peers += [(g, lax.rem(p + t, pieces)) for t in range(1, pieces)]
    for peer in peers:
        pl.semaphore_signal(barrier, inc=1, device_id=peer, device_id_type=MESH)
    pl.semaphore_wait(barrier, len(peers))


def remote(src, dst, sems, index, peer):
    return pltpu.make_async_remote_copy(
        src_ref=src,
        dst_ref=dst,
        send_sem=sems.at[(0,) + index],
        recv_sem=sems.at[(1,) + index],
        device_id=peer,
        device_id_type=MESH,
    )


def slabs_of(experts, owners, pieces, capacity, width):
    for t in range(pieces):
        for s in range(experts):
            for o in range(owners):
                rows = pl.ds((s * owners + o) * capacity, capacity)
                yield (t, s, o), (rows, pl.ds(t * width, width))


def dispatch_kernel(
    experts, owners, pieces, src, rows_out, out, local, direct, core, cross, cross_core
):
    g, p, c, k = place(experts, owners, pieces)
    greet(experts, owners, pieces)
    keep = pltpu.make_async_copy(src.at[c], out.at[p, c, k], local)
    keep.start()
    sends = {}
    for j in range(1, experts):
        e = lax.rem(c + j, experts)
        sends[j] = remote(src.at[e], out.at[p, c, k], direct, (j,), (e * owners + k, p))
        sends[j].start()
    to_core, to_piece, to_cross = [], {}, []
    for j in range(experts):
        s = lax.rem(c + experts - j, experts)
        if j == 0:
            keep.wait()
        else:
            sends[j].wait_recv()
        slab = out.at[p, s, k]
        for t in range(1, pieces):
            copy = remote(slab, slab, cross, (t, j), (g, lax.rem(p + t, pieces)))
            copy.start()
            to_piece[t, j] = copy
        for d in range(1, owners):
            peer = (c * owners + lax.rem(k + d, owners), p)
            copy = remote(slab, slab, core, (d, j), peer)
            copy.start()
            to_core.append(copy)
    for j in range(experts):
        s = lax.rem(c + experts - j, experts)
        for t in range(1, pieces):
            to_piece[t, j].wait_recv()
            slab = out.at[lax.rem(p + pieces - t, pieces), s, k]
            for d in range(1, owners):
                peer = (c * owners + lax.rem(k + d, owners), p)
                copy = remote(slab, slab, cross_core, (t, d, j), peer)
                copy.start()
                to_cross.append(copy)
    for copy in to_core + to_cross:
        copy.wait()
    for copy in list(sends.values()) + list(to_piece.values()):
        copy.wait_send()
    for slab, block in slabs_of(experts, owners, pieces, *src.shape[1:]):
        rows_out[block] = out[slab]


def collect_kernel(
    experts, owners, pieces, rows_in, out, part, near, leaving, arrived, final, core, cross, back
):
    g, p, c, k = place(experts, owners, pieces)
    greet(experts, owners, pieces)
    order = list(range(1, experts)) + [0]
    near_copies, cross_copies, back_copies = {}, {}, {}
    for slab, block in slabs_of(experts, owners, pieces, *out.shape[1:]):
        part[slab] = rows_in[block]
    for t in list(range(1, pieces)) + [0]:
        for j in order:
            s = lax.rem(c + j, experts)
            piece = lax.rem(p + t, pieces)
            for d in range(1, owners):
                other = lax.rem(k + d, owners)
                copy = remote(
                    part.at[piece, s, other],
                    near.at[d - 1, t, j],
                    core,
                    (d, t, j),
                    (c * owners + other, p),
                )
                copy.start()
                near_copies[d, t, j] = copy

    def chip_sum(t, j):
        total = part[lax.rem(p + t, pieces), lax.rem(c + j, experts), k].astype(jnp.float32)
        for d in range(1, owners):
            near_copies[d, t, j].wait_recv()
            total = total + near[d - 1, t, j].astype(jnp.float32)
        return total

    for j in order:
        for t in range(1, pieces):
            leaving[t - 1, j] = chip_sum(t, j).astype(leaving.dtype)
            copy = remote(
                leaving.at[t - 1, j],
                arrived.at[t - 1, j],
                cross,
                (t, j),
                (g, lax.rem(p + t, pieces)),
            )
            copy.start()
            cross_copies[t, j] = copy
    for j in order:
        total = chip_sum(0, j)
        for t in range(1, pieces):
            cross_copies[t, j].wait_recv()
            total = total + arrived[t - 1, j].astype(jnp.float32)
        if j == 0:
            out[c] = total.astype(out.dtype)
        else:
            final[j] = total.astype(final.dtype)
            peer = (lax.rem(c + j, experts) * owners + k, p)
            copy = remote(final.at[j], out.at[c], back, (j,), peer)
            copy.start()
            back_copies[j] = copy
    for copy in back_copies.values():
        copy.wait()
    for copy in list(near_copies.values()) + list(cross_copies.values()):
        copy.wait_send()


def dispatch(outgoing, owners, pieces):
    experts, capacity, width = outgoing.shape
    dma = pltpu.SemaphoreType.DMA
    return pl.pallas_call(
        partial(dispatch_kernel, experts, owners, pieces),
        out_shape=jax.ShapeDtypeStruct(
            (experts * owners * capacity, pieces * width), outgoing.dtype
        ),
        in_specs=[pl.BlockSpec(memory_space=pltpu.VMEM)],
        out_specs=pl.BlockSpec(memory_space=pltpu.VMEM),
        scratch_shapes=[
            pltpu.VMEM((pieces, experts, owners, capacity, width), outgoing.dtype),
            dma,
            dma((2, experts)),
            dma((2, owners, experts)),
            dma((2, pieces, experts)),
            dma((2, pieces, owners, experts)),
        ],
        compiler_params=pltpu.CompilerParams(
            collective_id=0, has_side_effects=True, vmem_limit_bytes=60 * 2**20
        ),
    )(outgoing)


def collect(part, experts, owners, pieces):
    capacity, width = part.shape[0] // (experts * owners), part.shape[1] // pieces
    dma = pltpu.SemaphoreType.DMA
    slabs = lambda *lead: pltpu.VMEM(lead + (capacity, width), part.dtype)
    return pl.pallas_call(
        partial(collect_kernel, experts, owners, pieces),
        out_shape=jax.ShapeDtypeStruct((experts, capacity, width), part.dtype),
        in_specs=[pl.BlockSpec(memory_space=pltpu.VMEM)],
        out_specs=pl.BlockSpec(memory_space=pltpu.VMEM),
        scratch_shapes=[
            slabs(pieces, experts, owners),
            slabs(max(owners - 1, 1), pieces, experts),
            slabs(max(pieces - 1, 1), experts),
            slabs(max(pieces - 1, 1), experts),
            slabs(experts),
            dma((2, owners, pieces, experts)),
            dma((2, pieces, experts)),
            dma((2, experts)),
        ],
        compiler_params=pltpu.CompilerParams(
            collective_id=1, has_side_effects=True, vmem_limit_bytes=60 * 2**20
        ),
    )(part)


def per_device(tokens, norm_gain, router_weight, expert_ids, gate_proj, up_proj, down_proj):
    tok_rows, local_width = tokens.shape
    experts = router_weight.shape[1]
    groups, pieces = lax.axis_size("grp"), lax.axis_size("tp")
    owners = groups // experts
    capacity = CAP
    start = lax.axis_index("tp") * local_width
    gain = lax.dynamic_slice_in_dim(norm_gain, start, local_width)
    router = lax.dynamic_slice_in_dim(router_weight, start, local_width, axis=0)
    values = tokens.astype(jnp.float32)
    squares = jnp.sum(values * values, axis=-1)
    squares = jnp.sum(lax.all_gather(squares, "tp"), axis=0)
    mean_square = (squares / (local_width * pieces))[:, None]
    normed = (values * lax.rsqrt(mean_square + epsilon) * gain).astype(jnp.bfloat16)
    logits = jnp.dot(normed, router, preferred_element_type=jnp.float32)
    logits = jnp.sum(lax.all_gather(logits, "tp"), axis=0)
    expert_iota = jnp.arange(experts, dtype=jnp.int32)[None, :]
    chosen_first = (expert_ids[:, 0:1] == expert_iota).astype(jnp.int32)
    chosen_second = (expert_ids[:, 1:2] == expert_iota).astype(jnp.int32)
    first_logit = jnp.sum(logits * chosen_first.astype(jnp.float32), axis=-1)
    second = jnp.sum(logits * chosen_second.astype(jnp.float32), axis=-1)
    gate_first = 1.0 / (1.0 + jnp.exp(second - first_logit))
    gate_second = 1.0 / (1.0 + jnp.exp(first_logit - second))
    gate_table = gate_first[:, None] * chosen_first.astype(jnp.float32) + gate_second[
        :, None
    ] * chosen_second.astype(jnp.float32)
    routed = chosen_first + chosen_second
    slot_index = jnp.cumsum(routed, axis=0) - 1
    slot_iota = jnp.arange(capacity, dtype=jnp.int32)
    slot_picks = (slot_index.T[:, None, :] == slot_iota[None, :, None]) & (
        routed.T[:, None, :] == 1
    )
    selector = slot_picks.astype(jnp.bfloat16)
    outgoing = jnp.einsum(
        "ect,td->ecd", selector, normed, preferred_element_type=jnp.float32
    ).astype(jnp.bfloat16)
    row_block = dispatch(outgoing, owners, pieces)
    gate_act = jnp.dot(row_block, gate_proj, preferred_element_type=jnp.float32)
    up_act = jnp.dot(row_block, up_proj, preferred_element_type=jnp.float32)
    hidden = (jax.nn.silu(gate_act) * up_act).astype(jnp.bfloat16)
    partial_out = jnp.dot(hidden, down_proj, preferred_element_type=jnp.float32).astype(
        jnp.bfloat16
    )
    summed = collect(partial_out, experts, owners, pieces).astype(jnp.float32)
    combine = slot_picks.astype(jnp.float32) * gate_table.T[:, None, :]
    mixed = jnp.einsum("ect,ecd->td", combine, summed, precision=lax.Precision.HIGHEST)
    return mixed.astype(jnp.bfloat16)


def solution(mesh):
    in_specs = (
        P("grp", "tp"),
        P(),
        P(),
        P("grp", None),
        P(None, ("grp", "tp")),
        P(None, ("grp", "tp")),
        P(("grp", "tp"), None),
    )
    out_specs = P("grp", "tp")
    return jax.shard_map(
        per_device, mesh=mesh, in_specs=in_specs, out_specs=out_specs, check_vma=False
    )
```

time: 309 us -> 149 us (0.48)
  blocking collectives: 122 us -> 6.96 us
  waiting for transfers between devices: 113 us -> 0 us
  Pallas kernels: 0 us -> 92.1 us
  between operations: 13.5 us -> 0.72 us
  local copies, waits for them, and re-layouts: 11.7 us -> 3.23 us
  starting transfers between devices: 6.51 us -> 0 us
    all_to_all x1 -> x0, blocking collectives: 111 us -> none  [per_device(): lax.all_to_all(outgoing, 'grp', split_axis=0, concat_axis=0, tiled=True)]
    pallas_call x0 -> x2, Pallas kernels: none -> 92.1 us  [the longest x1 47.3 us: collect(): pl.pallas_call(partial(collect_kernel, experts, owners, pieces), out_shap...]
    reduce_scatter x1 -> x0, waiting for transfers between devices: 59.9 us -> none  [expert_rows(): lax.psum_scatter(partial_out, 'tp', scatter_dimension=2, tiled=True)]
    all_to_all x1 -> x0, waiting for transfers between devices: 52.6 us -> none  [expert_rows(): lax.all_to_all(own_share, 'grp', split_axis=0, concat_axis=0, tiled=True)]
    reshape x2 -> x0, local copies, waits for them, and re-layouts: 10.2 us -> none  [the longest x1 5.13 us: expert_rows(): row_block = received.reshape(source_groups * slot_count, feature_width)]
    all_gather x1, blocking collectives: 10.9 us -> 3.2 us  [per_device(): logits = jnp.sum(lax.all_gather(logits, 'tp'), axis=0)]
    all_to_all x1 -> x0, starting transfers between devices: 6.51 us -> none  [expert_rows(): lax.all_to_all(own_share, 'grp', split_axis=0, concat_axis=0, tiled=True)]
    unnamed x0 -> x1, blocking collectives: none -> 3.75 us
  transfers between devices with their start and end apart: 2 -> 0, of which waited for: 2 -> 0; matrix products, arithmetic and copies ran while one was open for 0% -> 0% of each run, Pallas kernels for 0% -> 0%
where the time goes in v1:
time: 149 us
  Pallas kernels  92.1 us (62%)
  matrix products  44.6 us (30%)
  blocking collectives  6.96 us (5%)
  local copies, waits for them, and re-layouts  3.23 us (2%)
    pallas_call x1, Pallas kernels, collect(): pl.pallas_call(partial(collect_kernel, experts, owners, pieces), out_shap...  47.3 us
    pallas_call x1, Pallas kernels, dispatch(): pl.pallas_call(partial(dispatch_kernel, experts, owners, pieces), out_sha...  44.8 us
    dot_general x1, matrix products, per_device(): jnp.dot(hidden, down_proj, preferred_element_type=jnp.float32)  24.7 us
    dot_general x1, matrix products, per_device(): gate_act = jnp.dot(row_block, gate_proj, preferred_element_type=jnp.float32)  13.2 us
    unnamed x1, blocking collectives  3.75 us
    all_gather x1, blocking collectives, per_device(): logits = jnp.sum(lax.all_gather(logits, 'tp'), axis=0)  3.2 us

profile of v1, /device:TPU:13, one launch (start us, length us, event | category | flops | bytes accessed | tf_op | source)
XLA Modules:
  0.0 148.9 jit_solution(2890629006017018905)
XLA Ops:
  0.0 0.0 copy-start
  0.0 1.3 dynamic-slice
  1.9 1.2 fusion.8
  3.1 0.2 dynamic-update-slice
  3.4 3.8 %all-reduce = f32[128]{0:T(128)S(1)} all-reduce(f32[128]{0:T(128)S(1)} %dynamic-update-slice), channel_id=2, replica_groups=mesh['grp'=16,'tp'=2] {'tp'}, use_global_device_ids=true, to_apply=%add | all-reduce | flops 128 | bytes 1024
  7.1 0.1 reshape.131
  7.2 0.8 slice_bitcast_fusion.1
  8.0 0.7 dynamic_slice.6
  8.7 0.0 copy-done
  8.7 1.3 convolution_bitcast_fusion.1
  10.0 3.2 %all-gather.2 = f32[2,64,8]{1,2,0:T(8,128)S(1)} all-gather(f32[1,64,8]{1,2,0:T(8,128)S(1)} %convolution_bitcast_fusion.1), channel_id=3, replica_groups=mesh['grp'=16,'tp'=2] {'tp'}, dimensions={0}, use_global_device_ids=true | all-gather | bytes 6144 | tf_op jit(solution)/shard_map/all_gather | solution.py:226
  13.3 0.1 copy.9
  13.4 0.1 reduce_window_sum.11
  13.5 0.1 copy.10
  13.5 2.5 %convolution_convert_fusion.1.src = bf16[8,18,3072]{2,1,0:T(8,128)(2,1)} fusion(bf16[64,3072]{1,0:T(8,128)(2,1)} %param.7, f32[3072]{0:T(1024)S(1)} %dynamic_slice.6, f32[64]{0:T(128)S(1)} %add_rsqrt_fusion, s32[8,64]{1,0:T(8,128)S(1)} %copy.10, pred[8,64]{1,0:T(8,128)(4,1)S(1)} %fusion.31), kind=kOutput, calls=%fused_computation.1 | convolution fusion | flops 57870336 | bytes 1293056 | tf_op jit(solution)/shard_map/ect,td->ecd/dot_general | solution.py:244
  16.1 44.8 %shard_map.73 = bf16[288,6144]{1,0:T(8,128)(2,1)} custom-call(bf16[8,18,3072]{2,1,0:T(8,128)(2,1)} %convolution_convert_fusion.1.src), custom_call_target="tpu_custom_call" | custom-call | tf_op jit(solution)/shard_map/pallas_call | solution.py:165
  60.9 13.2 %fusion.36 = f32[288,2048]{1,0:T(8,128)S(1)} fusion(bf16[288,6144]{1,0:T(8,128)(2,1)} %shard_map.73, bf16[6144,2048]{1,0:T(8,128)(2,1)} %param.11), kind=kOutput, calls=%fused_computation.56 | convolution fusion | flops 7247757312 | bytes 31064064 | tf_op jit(solution)/shard_map/dot_general | solution.py:248
  74.1 0.0 copy-start.1
  74.1 24.7 %convolution_convert_fusion.rows_in = bf16[288,6144]{1,0:T(8,128)(2,1)} fusion(bf16[2048,6144]{1,0:T(8,128)(2,1)} %param.13, bf16[288,6144]{1,0:T(8,128)(2,1)} %shard_map.73, bf16[6144,2048]{1,0:T(8,128)(2,1)} %param.12, f32[288,2048]{1,0:T(8,128)S(1)} %fusion.36), kind=kOutput, calls=%fused_computation | convolution fusion | flops 14500823040 | bytes 59768832 | tf_op jit(solution)/shard_map/dot_general | solution.py:251
  98.8 47.3 %shard_map.74 = bf16[8,18,3072]{2,1,0:T(8,128)(2,1)} custom-call(bf16[288,6144]{1,0:T(8,128)(2,1)} %convolution_convert_fusion.rows_in), custom_call_target="tpu_custom_call" | custom-call | tf_op jit(solution)/shard_map/pallas_call | solution.py:190
  146.1 2.8 %fusion = bf16[64,3072]{1,0:T(8,128)(2,1)} fusion(bf16[8,18,3072]{2,1,0:T(8,128)(2,1)} %shard_map.74, f32[8,64]{1,0:T(8,128)S(1)} %fusion.30, s32[8,64]{1,0:T(8,128)S(1)} %copy.10, pred[8,64]{1,0:T(8,128)(4,1)S(1)} %fusion.31), kind=kOutput, calls=%fused_computation.3 | convolution fusion | flops 339962880 | bytes 1282560 | tf_op jit(solution)/shard_map/ect,ecd->td/dot_general | solution.py:256
  148.9 0.0 copy-done.1
  (10 shorter events, 0.1 us)
Async XLA Ops:
  0.0 8.7 %copy-start = (bf16[6144,8]{0,1:T(8,128)(2,1)S(1)}, bf16[6144,8]{0,1:T(8,128)(2,1)}, u32[]{:S(2)}) copy-start(bf16[6144,8]{0,1:T(8,128)(2,1)} %param.9) | copy-start | bytes 294916
  74.1 74.8 %copy-start.1 = (bf16[6144,8]{0,1:T(8,128)(2,1)S(1)}, bf16[6144,8]{0,1:T(8,128)(2,1)}, u32[]{:S(2)}) copy-start(bf16[6144,8]{0,1:T(8,128)(2,1)} %param.9) | copy-start | bytes 294916
